TPU v7x, 32 devices: a whole 2x2x4 slice. The times are simulated.
32 devices in a mesh: row: 2 (over x), col: 16 (over z, y, core).
Axes of the slice: x: 2, y: 2, z: 4, core: 2. Of those that a mesh axis runs over, the one named last changes fastest.
Arguments:
- ld_matrix: bfloat16 [32768, 32768], P('row', 'col'), may hold values from -0.23925781 to 0.23925781
- factor: float32 [32768, 256], P(('row', 'col')), may hold values from -0.24 to 0.24
- diag_values: bfloat16 [32768], P('col'), may hold values from 0.5 to 4
Outputs:
- factor_grad: float32 [32768, 256], P(('row', 'col'))
All inputs are finite; a program needn't handle non-finite values.
Results may differ from a plain program's by a relative error of at most 0.003.
Values may be sent and summed in bfloat16 or wider, within the bound.
A program may use at most 128 MiB of HBM per device.

v0:
```python
import jax
import jax.numpy as jnp
from jax import lax
from jax.sharding import PartitionSpec as P


def local(ld_matrix, factor, diag_values):
    n_row, n_col = (lax.axis_size("row"), lax.axis_size("col"))
    row_index, col_index = (lax.axis_index("row"), lax.axis_index("col"))
    factor_low = factor.astype(jnp.bfloat16)
    own, rank = factor.shape
    width = ld_matrix.shape[1]
    panel = jnp.zeros((width, rank), jnp.bfloat16)
    for k in range(n_row):
        pairs = [
            (n_row * c + (r + k) % n_row, r * n_col + c) for r in range(n_row) for c in range(n_col)
        ]
        piece = lax.ppermute(factor_low, ("row", "col"), pairs)
        at = lax.rem(row_index + k, n_row) * own
        panel = lax.dynamic_update_slice_in_dim(panel, piece, at, 0)
    gram = lax.dot_general(
        factor_low, factor_low, (((0,), (0,)), ((), ())), preferred_element_type=jnp.float32
    )
    gram = lax.psum(gram, ("row", "col"))
    part = jnp.dot(ld_matrix, panel, preferred_element_type=jnp.float32)
    per_row = n_col // n_row
    first = col_index % per_row * width
    scale = jnp.where(row_index == col_index // per_row, diag_values, 0).astype(jnp.float32)
    slab = lax.dynamic_slice_in_dim(part, first, width, 0)
    slab = slab - scale[:, None] * panel.astype(jnp.float32)
    part = lax.dynamic_update_slice_in_dim(part, slab, first, 0).astype(jnp.bfloat16)
    total = lax.psum_scatter(part, "col", scatter_dimension=0, tiled=True)
    model = jnp.dot(
        factor_low, gram, precision=lax.Precision.HIGHEST, preferred_element_type=jnp.float32
    )
    return 4.0 * (model - total.astype(jnp.float32))


def solution(mesh):
    in_specs = (P("row", "col"), P(("row", "col"), None), P("col"))
    out_specs = P(("row", "col"), None)
    return jax.shard_map(local, mesh=mesh, in_specs=in_specs, out_specs=out_specs, check_vma=False)
```

profile of v0, /device:TPU:0, one launch (start us, length us, event | category | flops | bytes accessed | tf_op | source)
XLA Modules:
  0.0 220.3 jit_solution(2321519786538181490)
XLA Ops:
  7.4 0.0 all-reduce.2.cloned.1.call-start
  7.4 1.4 copy.4
  8.8 0.7 collective-permute-start
  9.5 6.8 %collective-permute-start.1 = (bf16[1024,256]{0,1:T(8,128)(2,1)S(1)}, bf16[1024,256]{0,1:T(8,128)(2,1)S(1)}, u32[]{:S(2)}, u32[]{:S(2)}) collective-permute-start(bf16[1024,256]{0,1:T(8,128)(2,1)S(1)} %copy.4), channel_id=1, source_target_pairs={{1,0},{3,1},{5,2},{7,3},{9,4},{11,5},{13,6},{15,7},{17,8},{19,9},{... | collective-permute-start | bytes 1572872 | tf_op jit(solution)/shard_map/ppermute | solution.py:18
  16.3 1.0 fusion.1
  17.3 0.0 all-reduce.2.cloned.1.call-update
  17.4 0.0 reduce-scatter.2.cloned.1.call-start
  17.5 0.7 select_convert_fusion
  18.2 0.0 collective-permute-done
  18.2 0.1 broadcast_in_dim.8
  18.3 0.1 constant_dynamic-update-slice_fusion.1
  18.3 17.3 %collective-permute-done.1 = bf16[1024,256]{0,1:T(8,128)(2,1)S(1)} collective-permute-done((bf16[1024,256]{0,1:T(8,128)(2,1)S(1)}, bf16[1024,256]{0,1:T(8,128)(2,1)S(1)}, u32[]{:S(2)}, u32[]{:S(2)}) %collective-permute-start.1) | collective-permute-done | bytes 524320 | tf_op jit(solution)/shard_map/ppermute | solution.py:18
  35.7 32.1 %fusion.2 = f32[256,16384]{1,0:T(8,128)} fusion(bf16[2048,256]{0,1:T(8,128)(2,1)S(1)} %constant_dynamic-update-slice_fusion, bf16[16384,2048]{1,0:T(8,128)(2,1)} %param.3), kind=kOutput, calls=%fused_computation.8 | convolution fusion | flops 17179869184 | bytes 84934656 | tf_op jit(solution)/shard_map/dot_general | solution.py:25
  67.8 5.8 %copy.9 = f32[16384,256]{0,1:T(8,128)S(1)} copy(f32[16384,256]{0,1:T(8,128)} %bitcast.13) | data formatting | bytes 33554432
  73.7 2.0 fusion
  75.7 3.7 %convert_element_type.20 = bf16[16384,256]{0,1:T(8,128)(2,1)} convert(f32[16384,256]{0,1:T(8,128)S(1)} %fusion) | non-fusion elementwise | flops 4194304 | bytes 25165824 | tf_op jit(solution)/shard_map/convert_element_type | solution.py:31
  79.4 0.0 reduce-scatter.2.cloned.1.call-update
  79.5 99.7 %all-reduce.2.cloned.1.call-done = f32[256,256]{1,0:T(8,128)} async-done(((f32[256,256]{1,0:T(8,128)}), f32[256,256]{1,0:T(8,128)}) %all-reduce.2.cloned.1.call-update) | async-done | bytes 262160 | tf_op jit(solution)/shard_map/psum | solution.py:24
  179.1 1.6 convolution_bitcast_fusion
  180.7 29.7 %reduce-scatter.2.cloned.1.call-done = bf16[1024,256]{0,1:T(8,128)(2,1)} async-done(((bf16[16384,256]{0,1:T(8,128)(2,1)}), bf16[1024,256]{0,1:T(8,128)(2,1)}) %reduce-scatter.2.cloned.1.call-update) | async-done | bytes 524304 | tf_op jit(solution)/shard_map/reduce_scatter | solution.py:32
  210.4 1.2 subtract_multiply_fusion
  211.6 1.3 copy.5
  (1 shorter events, 0.0 us)
Async XLA Ops:
  7.4 171.8 %all-reduce.2.cloned.1.call-start = ((), (), s32[]{:S(2)}) async-start(), calls=%async_computation.1 | async-start | bytes 524288 | tf_op jit(solution)/shard_map/psum | solution.py:24
  8.8 9.4 %collective-permute-start = (bf16[1024,256]{0,1:T(8,128)(2,1)S(1)}, bf16[1024,256]{0,1:T(8,128)(2,1)S(1)}, u32[]{:S(2)}, u32[]{:S(2)}) collective-permute-start(bf16[1024,256]{0,1:T(8,128)(2,1)S(1)} %copy.4), channel_id=1, source_target_pairs={{0,0},{2,1},{4,2},{6,3},{8,4},{10,5},{12,6},{14,7},{16,8},{18,9},{... | collective-permute-start | bytes 1572872 | tf_op jit(solution)/shard_map/ppermute | solution.py:18
  9.5 26.1 %collective-permute-start.1 = (bf16[1024,256]{0,1:T(8,128)(2,1)S(1)}, bf16[1024,256]{0,1:T(8,128)(2,1)S(1)}, u32[]{:S(2)}, u32[]{:S(2)}) collective-permute-start(bf16[1024,256]{0,1:T(8,128)(2,1)S(1)} %copy.4), channel_id=1, source_target_pairs={{1,0},{3,1},{5,2},{7,3},{9,4},{11,5},{13,6},{15,7},{17,8},{19,9},{... | collective-permute-start | bytes 1572872 | tf_op jit(solution)/shard_map/ppermute | solution.py:18
  17.4 193.0 %reduce-scatter.2.cloned.1.call-start = ((), (), s32[]{:S(2)}) async-start(), calls=%async_computation.2 | async-start | bytes 8912896 | tf_op jit(solution)/shard_map/reduce_scatter | solution.py:32
Sparse Core Ops, SparseCore 0:
  17.5 161.5 all-reduce.1
Sparse Core Ops, SparseCore 1:
  79.5 130.8 reduce-scatter.1
where the time goes:
time: 221 us; the launch traced here: 220 us
  waiting for transfers between devices  147 us (67%)
  matrix products  34.7 us (16%)
  between operations  14.9 us (7%)
  local copies, waits for them, and re-layouts  8.77 us (4%)
  other arithmetic  7.63 us (3%)
  starting transfers between devices  7.54 us (3%)
    psum x1, waiting for transfers between devices, local(): gram = lax.psum(gram, ('row', 'col'))  99.7 us
    dot_general x1, matrix products, local(): part = jnp.dot(ld_matrix, panel, preferred_element_type=jnp.float32)  32.1 us
    reduce_scatter x1, waiting for transfers between devices, local(): total = lax.psum_scatter(part, 'col', scatter_dimension=0, tiled=True)  29.7 us
    ppermute x2, waiting for transfers between devices, local(): piece = lax.ppermute(factor_low, ('row', 'col'), pairs)  17.3 us
    ppermute x2, starting transfers between devices, local(): piece = lax.ppermute(factor_low, ('row', 'col'), pairs)  7.49 us
    unnamed x2, local copies, waits for them, and re-layouts  7.26 us
  transfers between devices with their start and end apart: 4, of which 3 were waited for; matrix products, arithmetic and copies ran while one was open for 21% of the time, Pallas kernels for 0%

commit v1 on v0

--- a/solution.py
+++ b/solution.py
@@ -21,7 +21,8 @@
     gram = lax.dot_general(
         factor_low, factor_low, (((0,), (0,)), ((), ())), preferred_element_type=jnp.float32
     )
-    gram = lax.psum(gram, ("row", "col"))
+    parts = lax.all_gather(gram, ("row", "col"))
+    gram = jnp.sum(parts, axis=0)
     part = jnp.dot(ld_matrix, panel, preferred_element_type=jnp.float32)
     per_row = n_col // n_row
     first = col_index % per_row * width

time: 221 us -> 239 us (1.081)
  waiting for transfers between devices: 147 us -> 161 us
  other arithmetic: 7.63 us -> 11.6 us
    psum x1 -> x0, waiting for transfers between devices: 99.7 us -> none  [local(): gram = lax.psum(gram, ('row', 'col'))]
    reduce_scatter x1, waiting for transfers between devices: 29.7 us -> 114 us  [local(): total = lax.psum_scatter(part, 'col', scatter_dimension=0, tiled=True)]
    all_gather x0 -> x1, waiting for transfers between devices: none -> 28.9 us  [local(): parts = lax.all_gather(gram, ('row', 'col'))]
    reduce_sum x0 -> x1, other arithmetic: none -> 3.93 us  [local(): gram = jnp.sum(parts, axis=0)]
where the time goes in v1:
time: 239 us; the launch traced here: 238 us
  waiting for transfers between devices  161 us (67%)
  matrix products  33.8 us (14%)
  between operations  14.9 us (6%)
  other arithmetic  11.6 us (5%)
  local copies, waits for them, and re-layouts  8.73 us (4%)
  starting transfers between devices  7.54 us (3%)
    reduce_scatter x1, waiting for transfers between devices, local(): total = lax.psum_scatter(part, 'col', scatter_dimension=0, tiled=True)  114 us
    dot_general x1, matrix products, local(): part = jnp.dot(ld_matrix, panel, preferred_element_type=jnp.float32)  32.1 us
    all_gather x1, waiting for transfers between devices, local(): parts = lax.all_gather(gram, ('row', 'col'))  28.9 us
    ppermute x2, waiting for transfers between devices, local(): piece = lax.ppermute(factor_low, ('row', 'col'), pairs)  18.4 us
    ppermute x2, starting transfers between devices, local(): piece = lax.ppermute(factor_low, ('row', 'col'), pairs)  7.49 us
    unnamed x2, local copies, waits for them, and re-layouts  7.21 us
  transfers between devices with their start and end apart: 4, of which 3 were waited for; matrix products, arithmetic and copies ran while one was open for 21% of the time, Pallas kernels for 0%

profile of v1, /device:TPU:0, one launch (start us, length us, event | category | flops | bytes accessed | tf_op | source)
XLA Modules:
  0.0 238.1 jit_solution(14066603708535846430)
XLA Ops:
  7.4 0.0 all-gather.3.cloned.1.call-start
  7.4 1.4 copy.4
  8.8 1.0 fusion.1
  9.8 0.0 all-gather.3.cloned.1.call-update
  9.9 0.0 reduce-scatter.2.cloned.1.call-start
  9.9 0.7 collective-permute-start
  10.6 6.8 %collective-permute-start.1 = (bf16[1024,256]{0,1:T(8,128)(2,1)S(1)}, bf16[1024,256]{0,1:T(8,128)(2,1)S(1)}, u32[]{:S(2)}, u32[]{:S(2)}) collective-permute-start(bf16[1024,256]{0,1:T(8,128)(2,1)S(1)} %copy.4), channel_id=1, source_target_pairs={{1,0},{3,1},{5,2},{7,3},{9,4},{11,5},{13,6},{15,7},{17,8},{19,9},{... | collective-permute-start | bytes 1572872 | tf_op jit(solution)/shard_map/ppermute | solution.py:18
  17.4 0.7 select_convert_fusion
  18.1 0.0 collective-permute-done
  18.1 0.1 broadcast_in_dim.8
  18.2 0.1 constant_dynamic-update-slice_fusion.1
  18.3 18.4 %collective-permute-done.1 = bf16[1024,256]{0,1:T(8,128)(2,1)S(1)} collective-permute-done((bf16[1024,256]{0,1:T(8,128)(2,1)S(1)}, bf16[1024,256]{0,1:T(8,128)(2,1)S(1)}, u32[]{:S(2)}, u32[]{:S(2)}) %collective-permute-start.1) | collective-permute-done | bytes 524320 | tf_op jit(solution)/shard_map/ppermute | solution.py:18
  36.7 32.1 %fusion.2 = f32[256,16384]{1,0:T(8,128)} fusion(bf16[2048,256]{0,1:T(8,128)(2,1)S(1)} %constant_dynamic-update-slice_fusion, bf16[16384,2048]{1,0:T(8,128)(2,1)} %param.3), kind=kOutput, calls=%fused_computation.8 | convolution fusion | flops 17179869184 | bytes 84934656 | tf_op jit(solution)/shard_map/dot_general | solution.py:26
  68.9 5.8 %copy.8 = f32[16384,256]{0,1:T(8,128)S(1)} copy(f32[16384,256]{0,1:T(8,128)} %bitcast.14) | data formatting | bytes 33554432
  74.7 2.0 fusion
  76.7 3.8 %convert_element_type.20 = bf16[16384,256]{0,1:T(8,128)(2,1)} convert(f32[16384,256]{0,1:T(8,128)S(1)} %fusion) | non-fusion elementwise | flops 4194304 | bytes 25165824 | tf_op jit(solution)/shard_map/convert_element_type | solution.py:32
  80.5 0.0 reduce-scatter.2.cloned.1.call-update
  80.5 28.9 %all-gather.3.cloned.1.call-done = f32[8192,256]{1,0:T(8,128)} async-done(((f32[256,256]{1,0:T(8,128)}), f32[8192,256]{1,0:T(8,128)}) %all-gather.3.cloned.1.call-update) | async-done | bytes 8388624 | tf_op jit(solution)/shard_map/all_gather | solution.py:24
  109.4 3.9 %reduce_sum.9 = f32[256,256]{1,0:T(8,128)S(1)} reduce(f32[32,256,256]{2,1,0:T(8,128)} %bitcast.15, f32[]{:T(128)} %constant.40.clone.1), dimensions={0}, to_apply=%region_0.0 | reduce | flops 2031616 | bytes 8650756 | tf_op jit(solution)/shard_map/reduce_sum | solution.py:25
  113.3 0.6 convolution_bitcast_fusion
  113.9 114.2 %reduce-scatter.2.cloned.1.call-done = bf16[1024,256]{0,1:T(8,128)(2,1)} async-done(((bf16[16384,256]{0,1:T(8,128)(2,1)}), bf16[1024,256]{0,1:T(8,128)(2,1)}) %reduce-scatter.2.cloned.1.call-update) | async-done | bytes 524304 | tf_op jit(solution)/shard_map/reduce_scatter | solution.py:33
  228.1 1.2 subtract_multiply_fusion
  229.3 1.3 copy.5
  (1 shorter events, 0.0 us)
Async XLA Ops:
  7.4 102.0 %all-gather.3.cloned.1.call-start = ((), (), s32[]{:S(2)}) async-start(), calls=%async_computation.2 | async-start | bytes 8650752 | tf_op jit(solution)/shard_map/all_gather | solution.py:24
  9.9 218.2 %reduce-scatter.2.cloned.1.call-start = ((), (), s32[]{:S(2)}) async-start(), calls=%async_computation.1 | async-start | bytes 8912896 | tf_op jit(solution)/shard_map/reduce_scatter | solution.py:33
  9.9 8.2 %collective-permute-start = (bf16[1024,256]{0,1:T(8,128)(2,1)S(1)}, bf16[1024,256]{0,1:T(8,128)(2,1)S(1)}, u32[]{:S(2)}, u32[]{:S(2)}) collective-permute-start(bf16[1024,256]{0,1:T(8,128)(2,1)S(1)} %copy.4), channel_id=1, source_target_pairs={{0,0},{2,1},{4,2},{6,3},{8,4},{10,5},{12,6},{14,7},{16,8},{18,9},{... | collective-permute-start | bytes 1572872 | tf_op jit(solution)/shard_map/ppermute | solution.py:18
  10.6 26.1 %collective-permute-start.1 = (bf16[1024,256]{0,1:T(8,128)(2,1)S(1)}, bf16[1024,256]{0,1:T(8,128)(2,1)S(1)}, u32[]{:S(2)}, u32[]{:S(2)}) collective-permute-start(bf16[1024,256]{0,1:T(8,128)(2,1)S(1)} %copy.4), channel_id=1, source_target_pairs={{1,0},{3,1},{5,2},{7,3},{9,4},{11,5},{13,6},{15,7},{17,8},{19,9},{... | collective-permute-start | bytes 1572872 | tf_op jit(solution)/shard_map/ppermute | solution.py:18
Sparse Core Ops, SparseCore 0:
  11.0 98.2 all-gather.2
Sparse Core Ops, SparseCore 1:
  80.6 147.5 reduce-scatter.1

commit v2 on v0

--- a/solution.py
+++ b/solution.py
@@ -21,7 +21,8 @@
     gram = lax.dot_general(
         factor_low, factor_low, (((0,), (0,)), ((), ())), preferred_element_type=jnp.float32
     )
-    gram = lax.psum(gram, ("row", "col"))
+    for axis in ("col", "row"):
+        gram = lax.psum(gram, axis)
     part = jnp.dot(ld_matrix, panel, preferred_element_type=jnp.float32)
     per_row = n_col // n_row
     first = col_index % per_row * width

time: 221 us -> 275 us (1.24)
  waiting for transfers between devices: 147 us -> 203 us
    reduce_scatter x1, waiting for transfers between devices: 29.7 us -> 103 us  [local(): total = lax.psum_scatter(part, 'col', scatter_dimension=0, tiled=True)]
    ppermute x2, waiting for transfers between devices: 17.3 us -> 0.01 us  [local(): piece = lax.ppermute(factor_low, ('row', 'col'), pairs)]
    psum x1 -> x2, waiting for transfers between devices: 99.7 us -> 99.8 us  [local(): gram = lax.psum(gram, axis)]
  transfers between devices with their start and end apart: 4 -> 5, of which waited for: 3 -> 2; matrix products, arithmetic and copies ran while one was open for 21% -> 17% of each run, Pallas kernels for 0% -> 0%
where the time goes in v2:
time: 275 us; the launch traced here: 274 us
  waiting for transfers between devices  203 us (74%)
  matrix products  34.7 us (13%)
  between operations  13.2 us (5%)
  local copies, waits for them, and re-layouts  8.71 us (3%)
  other arithmetic  7.63 us (3%)
  starting transfers between devices  7.58 us (3%)
    reduce_scatter x1, waiting for transfers between devices, local(): total = lax.psum_scatter(part, 'col', scatter_dimension=0, tiled=True)  103 us
    psum x2, waiting for transfers between devices, local(): gram = lax.psum(gram, axis)  99.8 us
    dot_general x1, matrix products, local(): part = jnp.dot(ld_matrix, panel, preferred_element_type=jnp.float32)  32.1 us
    ppermute x2, starting transfers between devices, local(): piece = lax.ppermute(factor_low, ('row', 'col'), pairs)  7.49 us
    unnamed x2, local copies, waits for them, and re-layouts  7.2 us
  transfers between devices with their start and end apart: 5, of which 2 were waited for; matrix products, arithmetic and copies ran while one was open for 17% of the time, Pallas kernels for 0%

profile of v2, /device:TPU:0, one launch (start us, length us, event | category | flops | bytes accessed | tf_op | source)
XLA Modules:
  0.0 274.4 jit_solution(16317564804554738598)
XLA Ops:
  6.5 0.0 all-reduce.3.cloned.1.call-start
  6.5 1.4 copy.4
  8.0 0.7 collective-permute-start
  8.7 6.8 %collective-permute-start.1 = (bf16[1024,256]{0,1:T(8,128)(2,1)S(1)}, bf16[1024,256]{0,1:T(8,128)(2,1)S(1)}, u32[]{:S(2)}, u32[]{:S(2)}) collective-permute-start(bf16[1024,256]{0,1:T(8,128)(2,1)S(1)} %copy.4), channel_id=1, source_target_pairs={{1,0},{3,1},{5,2},{7,3},{9,4},{11,5},{13,6},{15,7},{17,8},{19,9},{... | collective-permute-start | bytes 1572872 | tf_op jit(solution)/shard_map/ppermute | solution.py:18
  15.5 1.0 fusion.1
  16.5 0.0 all-reduce.3.cloned.1.call-update
  16.5 0.0 all-reduce.5.cloned.1.call-start
  16.6 0.7 select_convert_fusion
  17.3 99.8 %all-reduce.3.cloned.1.call-done = f32[256,256]{1,0:T(8,128)} async-done(((f32[256,256]{1,0:T(8,128)}), f32[256,256]{1,0:T(8,128)}) %all-reduce.3.cloned.1.call-update) | async-done | bytes 262160 | tf_op jit(solution)/shard_map/psum | solution.py:25
  117.1 0.0 all-reduce.5.cloned.1.call-update
  117.1 0.0 reduce-scatter.2.cloned.1.call-start
  117.2 0.0 collective-permute-done
  117.2 0.1 broadcast_in_dim.8
  117.3 0.1 constant_dynamic-update-slice_fusion.1
  117.4 0.0 collective-permute-done.1
  117.4 0.1 constant_dynamic-update-slice_fusion
  117.5 32.1 %fusion.2 = f32[256,16384]{1,0:T(8,128)} fusion(bf16[2048,256]{0,1:T(8,128)(2,1)S(1)} %constant_dynamic-update-slice_fusion, bf16[16384,2048]{1,0:T(8,128)(2,1)} %param.3), kind=kOutput, calls=%fused_computation.8 | convolution fusion | flops 17179869184 | bytes 84934656 | tf_op jit(solution)/shard_map/dot_general | solution.py:26
  149.5 5.8 %copy.10 = f32[16384,256]{0,1:T(8,128)S(1)} copy(f32[16384,256]{0,1:T(8,128)} %bitcast.13) | data formatting | bytes 33554432
  155.3 2.0 fusion
  157.3 3.7 %convert_element_type.20 = bf16[16384,256]{0,1:T(8,128)(2,1)} convert(f32[16384,256]{0,1:T(8,128)S(1)} %fusion) | non-fusion elementwise | flops 4194304 | bytes 25165824 | tf_op jit(solution)/shard_map/convert_element_type | solution.py:32
  161.1 0.0 reduce-scatter.2.cloned.1.call-update
  161.1 0.0 all-reduce.5.cloned.1.call-done
  161.1 1.6 convolution_bitcast_fusion
  162.7 102.7 %reduce-scatter.2.cloned.1.call-done = bf16[1024,256]{0,1:T(8,128)(2,1)} async-done(((bf16[16384,256]{0,1:T(8,128)(2,1)}), bf16[1024,256]{0,1:T(8,128)(2,1)}) %reduce-scatter.2.cloned.1.call-update) | async-done | bytes 524304 | tf_op jit(solution)/shard_map/reduce_scatter | solution.py:33
  265.4 1.2 subtract_multiply_fusion
  266.6 1.3 copy.5
Async XLA Ops:
  6.5 110.6 %all-reduce.3.cloned.1.call-start = ((), (), s32[]{:S(2)}) async-start(), calls=%async_computation.1 | async-start | bytes 524288 | tf_op jit(solution)/shard_map/psum | solution.py:25
  8.0 109.2 %collective-permute-start = (bf16[1024,256]{0,1:T(8,128)(2,1)S(1)}, bf16[1024,256]{0,1:T(8,128)(2,1)S(1)}, u32[]{:S(2)}, u32[]{:S(2)}) collective-permute-start(bf16[1024,256]{0,1:T(8,128)(2,1)S(1)} %copy.4), channel_id=1, source_target_pairs={{0,0},{2,1},{4,2},{6,3},{8,4},{10,5},{12,6},{14,7},{16,8},{18,9},{... | collective-permute-start | bytes 1572872 | tf_op jit(solution)/shard_map/ppermute | solution.py:18
  8.7 108.7 %collective-permute-start.1 = (bf16[1024,256]{0,1:T(8,128)(2,1)S(1)}, bf16[1024,256]{0,1:T(8,128)(2,1)S(1)}, u32[]{:S(2)}, u32[]{:S(2)}) collective-permute-start(bf16[1024,256]{0,1:T(8,128)(2,1)S(1)} %copy.4), channel_id=1, source_target_pairs={{1,0},{3,1},{5,2},{7,3},{9,4},{11,5},{13,6},{15,7},{17,8},{19,9},{... | collective-permute-start | bytes 1572872 | tf_op jit(solution)/shard_map/ppermute | solution.py:18
  16.5 144.6 %all-reduce.5.cloned.1.call-start = ((), (), s32[]{:S(2)}) async-start(), calls=%async_computation.2 | async-start | bytes 524288 | tf_op jit(solution)/shard_map/psum | solution.py:25
  117.1 148.2 %reduce-scatter.2.cloned.1.call-start = ((), (), s32[]{:S(2)}) async-start(), calls=%async_computation.3 | async-start | bytes 8912896 | tf_op jit(solution)/shard_map/reduce_scatter | solution.py:33
Sparse Core Ops, SparseCore 0:
  16.7 100.4 all-reduce.2
  119.4 23.7 all-reduce.4
  161.2 104.1 reduce-scatter.1
